TPU v7x, 32 devices: a whole 2x2x4 slice. The times are simulated.
32 devices in a mesh: grp: 2 (over y), lon: 4 (over x, core), lat: 4 (over z).
Axes of the slice: x: 2, y: 2, z: 4, core: 2. Of those that a mesh axis runs over, the one named last changes fastest.
Arguments:
- tracers: float32 [4, 64, 128, 128], P('grp', 'lat', 'lon'), parts along dimension 0, may hold values from -6 to 6
- adjoint_in: float32 [4, 64, 128, 128], P('grp', 'lat', 'lon'), parts along dimension 0, may hold values from -6 to 6
- shifts: int32 [2, 64], replicated, may hold values from 0 to 127, as said below
- fractions: float32 [2, 64], replicated, may hold values from 0.05 to 0.95
- meridional: float32 [2, 64, 128], P(None, None, 'lon'), may hold values from -0.9 to 0.9
Outputs:
- advected: float32 [4, 64, 128, 128], P('grp', 'lat', 'lon'), parts along dimension 0
- adjoint_out: float32 [4, 64, 128, 128], P('grp', 'lat', 'lon'), parts along dimension 0
There are 2 independent parts, one for each index of `grp`. A program takes and returns all parts, laid end to end along the dimension named above; an argument that names none is the same for every part. Nothing has to cross between parts.
Inputs may be any that keep to these rules, and one draw needn't show every extreme that they name: At row j, shifts lie below 1 + (127) d^2 / 63^2 with d = |2j - 63|.
All inputs are finite; a program needn't handle non-finite values.
Results may differ from a plain program's by a relative error of at most 0.0003.
Values sent between devices are 32-bit elements; how exact they have to be, the bound alone decides.
A program may use at most 128 MiB of HBM per device.

v0:
```python
import functools

import jax
import jax.numpy as jnp
from jax import lax
from jax.experimental import pallas as pl
from jax.experimental.pallas import tpu as pltpu
from jax.sharding import PartitionSpec as P

MESH = pl.DeviceIdType.MESH
SUB = 8
RIM = 3


def chunk_list(levels, rows, step):
    return [(lv, r0) for lv in range(levels) for r0 in range(0, rows, step)]


def reach(total_cells, total_rows, row):
    d = abs(2 * row + 1 - total_rows)
    return (total_cells - 1) * d * d // ((total_rows - 1) * (total_rows - 1))


def face_terms(v):
    size = jnp.abs(v)
    beta = v * (0.5 * size) * (1.0 - size * (2.0 / 3.0))
    return beta, 0.5 * v * v


def zonal_taps(c):
    b = 1.0 - c * (2.0 / 3.0)
    p = c * (1.0 - 0.5 * c - 1.5 * c * b)
    q = c * (0.5 * c - 1.5 * c * b)
    r = 3.0 * c * c * b
    d = p - q
    t = 1.0 / 12.0
    s = 7.0 / 12.0
    return (
        -t * q,
        s * q - t * d,
        r + t * p + s * d + s * q,
        1.0 - r - s * p + s * d - t * q,
        -s * p - t * d,
        t * p,
    )


def general(dims, *refs):
    levels, rows, cells, width, n_lon, n_lat, step = dims
    chunks = chunk_list(levels, rows, step)
    nq = len(chunks)
    tr, ad, shifts_in, fractions_in, mer_in, of, oa = refs[:7]
    gath = (refs[7 : 7 + nq], refs[7 + nq : 7 + 2 * nq])
    zb, ab, vb, taps, shifts, fractions, mer, loc, ssem, rsem, hs, hr = refs[7 + 2 * nq :]
    total_cells = cells * n_lon
    total_rows = rows * n_lat
    n_x = n_lon // 2

    me = lax.axis_index("lon")
    lat = lax.axis_index("lat")
    first = lat * rows
    core = lax.rem(me, 2)
    partner = me + 1 - 2 * core
    order = list(range(nq))

    own = []
    dup = []
    for q, (lv, r0) in enumerate(chunks):
        a = pltpu.make_async_copy(
            tr.at[lv, pl.ds(r0, step)], gath[0][q].at[:, pl.ds(0, cells)], loc.at[q]
        )
        a.start()
        own.append(a)
    adc = pltpu.make_async_copy(ad, ab.at[:, pl.ds(RIM, rows)], loc.at[2 * nq])
    adc.start()
    for q, (lv, r0) in enumerate(chunks):
        b = pltpu.make_async_copy(
            tr.at[lv, pl.ds(r0, step)],
            gath[0][q].at[:, pl.ds(total_cells, cells)],
            loc.at[nq + q],
        )
        b.start()
        dup.append(b)

    small = []
    for k, (source, target) in enumerate(
        ((shifts_in, shifts), (fractions_in, fractions), (mer_in, mer))
    ):
        d = pltpu.make_async_copy(source, target, loc.at[2 * nq + 1 + k])
        d.start()
        small.append(d)

    barrier = pltpu.get_barrier_semaphore()
    pl.semaphore_signal(barrier, inc=1, device_id={"lon": partner}, device_id_type=MESH)
    for dx in range(1, n_x):
        pl.semaphore_signal(
            barrier, inc=1, device_id={"lon": lax.rem(me + 2 * dx, n_lon)}, device_id_type=MESH
        )

    @pl.when(lat > 0)
    def _():
        pl.semaphore_signal(barrier, inc=1, device_id={"lat": lat - 1}, device_id_type=MESH)

    @pl.when(lat < n_lat - 1)
    def _():
        pl.semaphore_signal(barrier, inc=1, device_id={"lat": lat + 1}, device_id_type=MESH)

    inner = jnp.logical_and(lat > 0, lat < n_lat - 1)

    @pl.when(inner)
    def _():
        pl.semaphore_wait(barrier, n_x + 2)

    @pl.when(jnp.logical_not(inner))
    def _():
        pl.semaphore_wait(barrier, n_x + min(n_lat - 1, 1))

    def lat_copies(buf, k):
        down = pltpu.make_async_remote_copy(
            buf.at[:, pl.ds(RIM, RIM)],
            buf.at[:, pl.ds(RIM + rows, RIM)],
            hs.at[k, 0],
            hr.at[k, 0],
            device_id={"lat": lat - 1},
            device_id_type=MESH,
        )
        up = pltpu.make_async_remote_copy(
            buf.at[:, pl.ds(rows, RIM)],
            buf.at[:, pl.ds(0, RIM)],
            hs.at[k, 1],
            hr.at[k, 1],
            device_id={"lat": lat + 1},
            device_id_type=MESH,
        )
        return down, up

    def lat_start(buf, k):
        down, up = lat_copies(buf, k)

        @pl.when(lat > 0)
        def _():
            down.start()

        @pl.when(lat < n_lat - 1)
        def _():
            up.start()

    def lat_wait(buf, k):
        down, up = lat_copies(buf, k)

        @pl.when(lat > 0)
        def _():
            down.wait_send()
            up.wait_recv()

        @pl.when(lat < n_lat - 1)
        def _():
            up.wait_send()
            down.wait_recv()

    def x_copy(a, q, dx, span):
        lo, hi = span
        return pltpu.make_async_remote_copy(
            gath[a][q].at[:, pl.ds(lo, hi - lo)],
            gath[a][q].at[:, pl.ds((n_lon - 2 * dx) * cells + lo, hi - lo)],
            ssem.at[a, q, dx],
            rsem.at[a, q, dx],
            device_id={"lon": lax.rem(me + 2 * dx, n_lon)},
            device_id_type=MESH,
        )

    def core_copy(a, q, dx, span):
        lo, hi = span
        source = ((n_lon - 2 * dx) % n_lon) * cells + lo
        slot = lax.rem(2 * n_lon - 2 * dx + 2 * core - 1, n_lon)
        return pltpu.make_async_remote_copy(
            gath[a][q].at[:, pl.ds(source, hi - lo)],
            gath[a][q].at[:, pl.ds(pl.multiple_of(slot * cells + lo, SUB), hi - lo)],
            ssem.at[a, q, n_x + dx],
            rsem.at[a, q, n_x + dx],
            device_id={"lon": partner},
            device_id_type=MESH,
        )

    whole = (0, cells)

    def gather_start(a, q):
        for dx in range(1, n_x):
            x_copy(a, q, dx, whole).start()
        core_copy(a, q, 0, whole).start()

    def relay(a, q):
        for dx in range(1, n_x):
            x_copy(a, q, dx, whole).wait_recv()
            core_copy(a, q, dx, whole).start()

    def gather_finish(a, q):
        for dx in range(n_x):
            core_copy(a, q, dx, whole).wait_recv()

    def gather_drain(a, q):
        for dx in range(n_x):
            core_copy(a, q, dx, whole).wait_send()
        for dx in range(1, n_x):
            x_copy(a, q, dx, whole).wait_send()

    adc.wait()
    lat_start(ab, 0)
    for q in range(nq):
        own[q].wait()
        gather_start(0, q)

    @pl.when(lat == 0)
    def _():
        for buf in (ab, zb):
            buf[:, pl.ds(0, RIM)] = jnp.zeros((levels, RIM, cells, width), jnp.float32)

    @pl.when(lat == n_lat - 1)
    def _():
        for buf in (ab, zb):
            buf[:, pl.ds(RIM + rows, RIM)] = jnp.zeros((levels, RIM, cells, width), jnp.float32)

    for d in small:
        d.wait()
    faces = rows + 5
    lanes = lax.broadcasted_iota(jnp.int32, (cells, total_rows), 1)
    for lv in range(levels):

        @pl.loop(0, faces)
        def _(f):
            row = first + f - 2
            chosen = jnp.logical_and(lanes == row, lanes > 0)
            column = jnp.sum(jnp.where(chosen, mer[lv], 0.0), axis=1, keepdims=True)
            vb[lv, f] = jnp.broadcast_to(column, (cells, width))

        @pl.loop(0, rows)
        def _(r):
            for k, t in enumerate(zonal_taps(fractions[lv, first + r])):
                taps[(lv * rows + r) * 6 + k] = t

    lat_wait(ab, 0)
    for lv in range(levels):

        @pl.loop(0, cells // SUB)
        def _(c):
            at = pl.ds(pl.multiple_of(c * SUB, SUB), SUB)
            ev, q6b, dqb, eb = {}, {}, {}, {}
            carry = None
            y = {r: ab[lv, r + RIM, at, :] for r in range(-3, -1)}
            for f in range(-2, rows + 3):
                y[f] = ab[lv, f + RIM, at, :]
                v = vb[lv, f + 2, at, :]
                north = v > 0.0
                beta, gamma = face_terms(v)
                change = y[f] - y[f - 1]
                ev[f] = v * change
                b = beta * change
                g = -gamma * change
                bn, gn = jnp.where(north, b, 0.0), jnp.where(north, g, 0.0)
                if carry is not None:
                    q6b[f - 1] = bn + carry[0]
                    dqb[f - 1] = gn + carry[1]
                carry = (b - bn, g - gn)
                h = f - 1
                if h >= -1:
                    eb[h] = ev[h] - 3.0 * (q6b[h - 1] + q6b[h]) + (dqb[h - 1] - dqb[h])
                r = h - 2
                if r >= 0:
                    value = (
                        y[r]
                        + 6.0 * q6b[r]
                        + (7.0 / 12.0) * (eb[r] + eb[r + 1])
                        - (1.0 / 12.0) * (eb[r - 1] + eb[r + 2])
                    )
                    q = lv * (rows // step) + r // step
                    gath[1][q][r % step, at, :] = value
                    gath[1][q][
                        r % step, pl.ds(pl.multiple_of(total_cells + c * SUB, SUB), SUB), :
                    ] = value

        for q, (l2, _r) in enumerate(chunks):
            if l2 == lv:
                gather_start(1, q)

    def sweep(a, q, sink, sink_row, sign):
        lv, r0 = chunks[q]
        buf = gath[a][q]

        @pl.loop(0, step)
        def _(r):
            buf[r, pl.ds(total_cells + cells, SUB), :] = buf[r, pl.ds(cells, SUB), :]
            shift = shifts[lv, first + r0 + r]
            if sign < 0:
                start = lax.rem(2 * total_cells - shift - 3, total_cells)
            else:
                start = lax.rem(2 * total_cells + shift - 2, total_cells)
            base = (lv * rows + r0 + r) * 6
            w = [taps[base + k] for k in range(6)]
            if sign > 0:
                w = w[::-1]
            for c in range(cells // SUB):
                total = None
                for k in range(6):
                    term = w[k] * buf[r, pl.ds(start + c * SUB + k, SUB), :]
                    total = term if total is None else total + term
                sink[lv, sink_row + r0 + r, pl.ds(c * SUB, SUB), :] = total

    for b in dup:
        b.wait()
    for i, q in enumerate(order):
        relay(0, q)
        if i > 0:
            gather_finish(0, order[i - 1])
            sweep(0, order[i - 1], zb, RIM, -1)
    gather_finish(0, order[-1])
    sweep(0, order[-1], zb, RIM, -1)
    lat_start(zb, 1)

    relay(1, order[0])
    lat_wait(zb, 1)

    for lv in range(levels):

        @pl.loop(0, cells // SUB)
        def _(c):
            at = pl.ds(pl.multiple_of(c * SUB, SUB), SUB)
            z = {r: zb[lv, r + RIM, at, :] for r in range(-3, 0)}
            e, q6, dq, flux = {}, {}, {}, {}
            for f in range(-1, rows + 2):
                z[f + 1] = zb[lv, f + 1 + RIM, at, :]
                e[f] = (7.0 / 12.0) * (z[f - 1] + z[f]) - (1.0 / 12.0) * (z[f - 2] + z[f + 1])
                u = f - 1
                if u >= -1:
                    q6[u] = 6.0 * z[u] - 3.0 * (e[u] + e[f])
                    dq[u] = e[f] - e[u]
                if u >= 0:
                    v = vb[lv, u + 2, at, :]
                    north = v > 0.0
                    beta, gamma = face_terms(v)
                    flux[u] = (
                        v * e[u]
                        + beta * jnp.where(north, q6[u - 1], q6[u])
                        - gamma * jnp.where(north, dq[u - 1], dq[u])
                    )
                if u >= 1:
                    of[lv, u - 1, at, :] = z[u - 1] - flux[u] + flux[u - 1]

    def finish_adjoint(q):
        lv, r0 = chunks[q]
        gather_finish(1, q)
        sweep(1, q, oa, 0, 1)

    for i in range(1, nq):
        relay(1, order[i])
        finish_adjoint(order[i - 1])
    finish_adjoint(order[-1])

    for a in range(2):
        for q in range(nq):
            gather_drain(a, q)


HEAD, TAIL = 0, 1


def fits(rows, cells, n_lon, n_lat):
    if n_lon != 4 or n_lat != 4 or rows % 4 or cells % SUB:
        return False
    return reach(cells * n_lon, rows * n_lat, rows) + RIM <= cells + SUB


def detours(levels, rows, step):
    per = rows // step
    return ((1, 2, per + 2), (1, 2, per + 2))


def pack_plan(rows, cells, n_lon, n_lat, a, side):
    big = (side == TAIL) == (a == 0)
    slots = []
    at = SUB
    for k in range(rows):
        s = RIM - 1
        if big:
            s = min(reach(cells * n_lon, rows * n_lat, rows + k) + RIM, cells)
        if s >= SUB:
            begins = list(range(0, s - SUB + 1, SUB))
            if s % SUB:
                begins.append(s - SUB)
            shift = cells - s if side == TAIL else 0
            slots.append([(shift + b, at + b) for b in begins])
        elif side == TAIL:
            slots.append([(cells - SUB, at + s - SUB)])
        else:
            slots.append([(0, at)])
        at += s
    long = -(-(at - SUB) // SUB) * SUB
    return slots, long


def pack_room(rows, cells, n_lon, n_lat):
    return 2 * SUB + max(
        pack_plan(rows, cells, n_lon, n_lat, a, side)[1] for a in range(2) for side in (HEAD, TAIL)
    )


def paired(dims, *refs):
    levels, rows, cells, width, n_lon, n_lat, step, det = dims
    chunks = chunk_list(levels, rows, step)
    nq = len(chunks)
    per = rows // step
    tr, ad, shifts_in, fractions_in, mer_in, of, oa = refs[:7]
    gath = (refs[7 : 7 + nq], refs[7 + nq : 7 + 2 * nq])
    zb, ab, vb, taps, shifts, fractions, mer, held = refs[7 + 2 * nq : 15 + 2 * nq]
    sendp, recvp, sendx, recvx, loc, ssem, rsem, hs, hr, vs, vr, ps, pr = refs[15 + 2 * nq :]
    total_cells = cells * n_lon
    total_rows = rows * n_lat

    me = lax.axis_index("lon")
    lat = lax.axis_index("lat")
    first = lat * rows
    core = lax.rem(me, 2)
    partner = me + 1 - 2 * core
    beside = lax.rem(me + 2, n_lon)
    joint = lax.rem(me + n_lon + 2 * core - 1, n_lon)
    mate = lat + 1 - 2 * lax.rem(lat, 2)
    middle = jnp.logical_and(lat > 0, lat < n_lat - 1)
    polar = jnp.logical_not(middle)

    own = []
    dup = []
    for q, (lv, r0) in enumerate(chunks):
        a = pltpu.make_async_copy(
            tr.at[lv, pl.ds(r0, step)], gath[0][q].at[:, pl.ds(0, cells)], loc.at[q]
        )
        a.start()
        own.append(a)
    adc = pltpu.make_async_copy(ad, ab.at[:, pl.ds(RIM, rows)], loc.at[2 * nq])
    adc.start()
    small = []
    for k, (source, target) in enumerate(
        ((shifts_in, shifts), (fractions_in, fractions), (mer_in, mer))
    ):
        d = pltpu.make_async_copy(source, target, loc.at[2 * nq + 1 + k])
        d.start()
        small.append(d)
    for q, (lv, r0) in enumerate(chunks):
        b = pltpu.make_async_copy(
            tr.at[lv, pl.ds(r0, step)],
            gath[0][q].at[:, pl.ds(total_cells, cells)],
            loc.at[nq + q],
        )
        b.start()
        dup.append(b)

    barrier = pltpu.get_barrier_semaphore()

    def greet(**place):
        pl.semaphore_signal(barrier, inc=1, device_id=place, device_id_type=MESH)

    greet(lon=partner)
    greet(lon=beside)
    greet(lon=beside, lat=mate)

    @pl.when(lat > 0)
    def _():
        greet(lat=lat - 1)

    @pl.when(lat < n_lat - 1)
    def _():
        greet(lat=lat + 1)

    @pl.when(middle)
    def _():
        greet(lon=joint)
        pl.semaphore_wait(barrier, 6)

    @pl.when(polar)
    def _():
        pl.semaphore_wait(barrier, 4)

    def remote(source, target, send, recv, **place):
        return pltpu.make_async_remote_copy(
            source, target, send, recv, device_id=place, device_id_type=MESH
        )

    def lat_copies(buf, k):
        down = remote(
            buf.at[:, pl.ds(RIM, RIM)],
            buf.at[:, pl.ds(RIM + rows, RIM)],
            hs.at[k, 0],
            hr.at[k, 0],
            lat=lat - 1,
        )
        up = remote(
            buf.at[:, pl.ds(rows, RIM)], buf.at[:, pl.ds(0, RIM)], hs.at[k, 1], hr.at[k, 1], lat=lat + 1
        )
        return down, up

    def lat_start(buf, k):
        down, up = lat_copies(buf, k)

        @pl.when(lat > 0)
        def _():
            down.start()

        @pl.when(lat < n_lat - 1)
        def _():
            up.start()

    def lat_wait(buf, k):
        down, up = lat_copies(buf, k)

        @pl.when(lat > 0)
        def _():
            down.wait_send()
            up.wait_recv()

        @pl.when(lat < n_lat - 1)
        def _():
            up.wait_send()
            down.wait_recv()

    own_block = pl.ds(0, cells)
    far_block = pl.ds((n_lon - 2) * cells, cells)

    def x_copy(a, q):
        g = gath[a][q]
        return remote(
            g.at[:, own_block], g.at[:, far_block], ssem.at[a, q, 0], rsem.at[a, q, 0], lon=beside
        )

    def core_copy(a, q, dx):
        g = gath[a][q]
        source = ((n_lon - 2 * dx) % n_lon) * cells
        slot = lax.rem(2 * n_lon - 2 * dx + 2 * core - 1, n_lon)
        return remote(
            g.at[:, pl.ds(source, cells)],
            g.at[:, pl.ds(pl.multiple_of(slot * cells, SUB), cells)],
            ssem.at[a, q, 1 + dx],
            rsem.at[a, q, 1 + dx],
            lon=partner,
        )

    def out_copy(a, q):
        i = det[a].index(q)
        return remote(
            gath[a][q].at[:, own_block],
            held.at[a, i],
            vs.at[a, i, 0],
            vr.at[a, i, 0],
            lon=beside,
            lat=mate,
        )

    def on_copy(a, q):
        i = det[a].index(q)
        return remote(
            held.at[a, i], gath[a][q].at[:, far_block], vs.at[a, i, 1], vr.at[a, i, 1], lat=mate
        )

    def far_send(a, q):
        return out_copy(a, q) if q in det[a] else x_copy(a, q)

    def far_recv(a, q):
        return on_copy(a, q) if q in det[a] else x_copy(a, q)

    plans = [[pack_plan(rows, cells, n_lon, n_lat, a, side) for side in (HEAD, TAIL)] for a in range(2)]
    ring = (cells, (n_lon - 1) * cells)
    spill = [
        k for k in range(rows) if reach(total_cells, total_rows, rows + k) + RIM > cells
    ]
    last = (cells - SUB, 0)

    def place_of(lv, k, south):
        r = k if south else rows - 1 - k
        return lv * per + r // step, r % step

    def by_half(act):
        for south in (True, False):

            @pl.when(lat == (1 if south else n_lat - 2))
            def _():
                act(south)

    def pack_copy(a, lv, side):
        long = plans[a][side][1]
        return remote(
            sendp.at[a, lv, pl.ds(SUB, long)],
            recvp.at[a, lv, pl.ds(SUB, long)],
            ps.at[a, lv],
            pr.at[a, lv],
            lon=joint,
        )

    def few_copy(a):
        return remote(sendx.at[a], recvx.at[a], ps.at[a, levels], pr.at[a, levels], lon=beside)

    def pack_send(a, lv):
        for side in (HEAD, TAIL):

            @pl.when(core == side)
            def _():
                def fill(south):
                    order = range(rows) if side == HEAD else reversed(range(rows))
                    for k in order:
                        q, j = place_of(lv, k, south)
                        for source, target in plans[a][side][0][k]:
                            sendp[a, lv, pl.ds(target, SUB), :] = gath[a][q][j, pl.ds(source, SUB), :]

                by_half(fill)
                pack_copy(a, lv, side).start()

        if spill:

            def few(south):
                q, j = place_of(lv, spill[0], south)
                sendx[a, pl.ds(lv * SUB, SUB), :] = gath[a][q][j, pl.ds(last[a], SUB), :]

            by_half(few)
            if lv == levels - 1:
                few_copy(a).start()

    def pack_take(a, lv):
        for side in (HEAD, TAIL):

            @pl.when(core == 1 - side)
            def _():
                pack_copy(a, lv, side).wait_recv()

                def empty(south):
                    for k in range(rows):
                        q, j = place_of(lv, k, south)
                        for source, target in plans[a][side][0][k]:
                            gath[a][q][j, pl.ds(ring[side] + source, SUB), :] = recvp[
                                a, lv, pl.ds(target, SUB), :
                            ]

                by_half(empty)

        if spill:
            if lv == 0:
                few_copy(a).wait_recv()

            def few(south):
                q, j = place_of(lv, spill[0], south)
                gath[a][q][j, pl.ds(2 * cells + last[a], SUB), :] = recvx[a, pl.ds(lv * SUB, SUB), :]

            by_half(few)

    def pass_on(a, q):
        out_copy(a, q).wait_recv()
        on_copy(a, q).start()

    def send_level(a, lv):
        for q in range(lv * per, (lv + 1) * per):
            core_copy(a, q, 0).start()

            @pl.when(polar)
            def _():
                far_send(a, q).start()

        @pl.when(middle)
        def _():
            pack_send(a, lv)

    adc.wait()
    lat_start(ab, 0)
    for lv in range(levels):
        for q in range(lv * per, (lv + 1) * per):
            own[q].wait()
        send_level(0, lv)

    @pl.when(lat == 0)
    def _():
        for buf in (ab, zb):
            buf[:, pl.ds(0, RIM)] = jnp.zeros((levels, RIM, cells, width), jnp.float32)

    @pl.when(lat == n_lat - 1)
    def _():
        for buf in (ab, zb):
            buf[:, pl.ds(RIM + rows, RIM)] = jnp.zeros((levels, RIM, cells, width), jnp.float32)

    for d in small:
        d.wait()
    faces = rows + 5
    lanes = lax.broadcasted_iota(jnp.int32, (cells, total_rows), 1)
    for lv in range(levels):

        @pl.loop(0, faces)
        def _(f):
            row = first + f - 2
            chosen = jnp.logical_and(lanes == row, lanes > 0)
            column = jnp.sum(jnp.where(chosen, mer[lv], 0.0), axis=1, keepdims=True)
            vb[lv, f] = jnp.broadcast_to(column, (cells, width))

        @pl.loop(0, rows)
        def _(r):
            for k, t in enumerate(zonal_taps(fractions[lv, first + r])):
                taps[(lv * rows + r) * 6 + k] = t

    lat_wait(ab, 0)
    for lv in range(levels):

        @pl.loop(0, cells // SUB)
        def _(c):
            at = pl.ds(pl.multiple_of(c * SUB, SUB), SUB)
            ev, q6b, dqb, eb = {}, {}, {}, {}
            carry = None
            y = {r: ab[lv, r + RIM, at, :] for r in range(-3, -1)}
            for f in range(-2, rows + 3):
                y[f] = ab[lv, f + RIM, at, :]
                v = vb[lv, f + 2, at, :]
                north = v > 0.0
                beta, gamma = face_terms(v)
                change = y[f] - y[f - 1]
                ev[f] = v * change
                b = beta * change
                g = -gamma * change
                bn, gn = jnp.where(north, b, 0.0), jnp.where(north, g, 0.0)
                if carry is not None:
                    q6b[f - 1] = bn + carry[0]
                    dqb[f - 1] = gn + carry[1]
                carry = (b - bn, g - gn)
                h = f - 1
                if h >= -1:
                    eb[h] = ev[h] - 3.0 * (q6b[h - 1] + q6b[h]) + (dqb[h - 1] - dqb[h])
                r = h - 2
                if r >= 0:
                    value = (
                        y[r]
                        + 6.0 * q6b[r]
                        + (7.0 / 12.0) * (eb[r] + eb[r + 1])
                        - (1.0 / 12.0) * (eb[r - 1] + eb[r + 2])
                    )
                    q = lv * per + r // step
                    gath[1][q][r % step, at, :] = value
                    gath[1][q][
                        r % step, pl.ds(pl.multiple_of(total_cells + c * SUB, SUB), SUB), :
                    ] = value

        send_level(1, lv)

    def sweep(a, q, sink, sink_row, sign):
        lv, r0 = chunks[q]
        buf = gath[a][q]

        @pl.loop(0, step)
        def _(r):
            buf[r, pl.ds(total_cells + cells, SUB), :] = buf[r, pl.ds(cells, SUB), :]
            shift = shifts[lv, first + r0 + r]
            if sign < 0:
                start = lax.rem(2 * total_cells - shift - 3, total_cells)
            else:
                start = lax.rem(2 * total_cells + shift - 2, total_cells)
            base = (lv * rows + r0 + r) * 6
            w = [taps[base + k] for k in range(6)]
            if sign > 0:
                w = w[::-1]
            for c in range(cells // SUB):
                total = None
                for k in range(6):
                    term = w[k] * buf[r, pl.ds(start + c * SUB + k, SUB), :]
                    total = term if total is None else total + term
                sink[lv, sink_row + r0 + r, pl.ds(c * SUB, SUB), :] = total

    def finish(a, q):
        for dx in range(2):
            core_copy(a, q, dx).wait_recv()
        if a == 0:
            sweep(0, q, zb, RIM, -1)
        else:
            sweep(1, q, oa, 0, 1)

    def relay(a, q):
        far_recv(a, q).wait_recv()
        core_copy(a, q, 1).start()

    def polar_finish(a):
        order = [q for q in range(nq) if q not in det[a]] + list(det[a])
        for i, q in enumerate(order):
            relay(a, q)
            if i > 0:
                finish(a, order[i - 1])
        finish(a, order[-1])

    def middle_finish(a):
        for lv in range(levels):
            pack_take(a, lv)
            for q in range(lv * per, (lv + 1) * per):
                core_copy(a, q, 0).wait_recv()
                if a == 0:
                    sweep(0, q, zb, RIM, -1)
                else:
                    sweep(1, q, oa, 0, 1)

    for b in dup:
        b.wait()

    @pl.when(polar)
    def _():
        polar_finish(0)

    @pl.when(middle)
    def _():
        middle_finish(0)

    lat_start(zb, 1)

    @pl.when(middle)
    def _():
        for q in det[0]:
            pass_on(0, q)
        middle_finish(1)
        for q in det[1]:
            pass_on(1, q)

    lat_wait(zb, 1)

    for lv in range(levels):

        @pl.loop(0, cells // SUB)
        def _(c):
            at = pl.ds(pl.multiple_of(c * SUB, SUB), SUB)
            z = {r: zb[lv, r + RIM, at, :] for r in range(-3, 0)}
            e, q6, dq, flux = {}, {}, {}, {}
            for f in range(-1, rows + 2):
                z[f + 1] = zb[lv, f + 1 + RIM, at, :]
                e[f] = (7.0 / 12.0) * (z[f - 1] + z[f]) - (1.0 / 12.0) * (z[f - 2] + z[f + 1])
                u = f - 1
                if u >= -1:
                    q6[u] = 6.0 * z[u] - 3.0 * (e[u] + e[f])
                    dq[u] = e[f] - e[u]
                if u >= 0:
                    v = vb[lv, u + 2, at, :]
                    north = v > 0.0
                    beta, gamma = face_terms(v)
                    flux[u] = (
                        v * e[u]
                        + beta * jnp.where(north, q6[u - 1], q6[u])
                        - gamma * jnp.where(north, dq[u - 1], dq[u])
                    )
                if u >= 1:
                    of[lv, u - 1, at, :] = z[u - 1] - flux[u] + flux[u - 1]

    @pl.when(polar)
    def _():
        polar_finish(1)

    for a in range(2):
        for q in range(nq):
            core_copy(a, q, 0).wait_send()

            @pl.when(polar)
            def _():
                far_send(a, q).wait_send()
                core_copy(a, q, 1).wait_send()

        @pl.when(middle)
        def _():
            for q in det[a]:
                on_copy(a, q).wait_send()
            for lv in range(levels):
                for side in (HEAD, TAIL):

                    @pl.when(core == side)
                    def _():
                        pack_copy(a, lv, side).wait_send()

            if spill:
                few_copy(a).wait_send()


def store(f_in, a_in, f_out, a_out, sem):
    one = pltpu.make_async_copy(f_in, f_out, sem.at[0])
    two = pltpu.make_async_copy(a_in, a_out, sem.at[1])
    one.start()
    two.start()
    one.wait()
    two.wait()


def local(tracers, adjoint_in, shifts, fractions, meridional):
    levels, rows, cells, width = tracers.shape
    n_lon, n_lat = lax.axis_size("lon"), lax.axis_size("lat")
    n_x = n_lon // 2
    pair = fits(rows, cells, n_lon, n_lat)
    step = max(1, rows // (4 if pair else 2))
    nq = levels * (rows // step)
    dma = pltpu.SemaphoreType.DMA
    block = pltpu.VMEM((step, (n_lon + 1) * cells + SUB, width), jnp.float32)
    banded = pltpu.VMEM((levels, rows + 2 * RIM, cells, width), jnp.float32)
    scratch = [block] * (2 * nq) + [
        banded,
        banded,
        pltpu.VMEM((levels, rows + 5, cells, width), jnp.float32),
        pltpu.SMEM((levels * rows * 6,), jnp.float32),
        pltpu.SMEM(shifts.shape, jnp.int32),
        pltpu.SMEM(fractions.shape, jnp.float32),
        pltpu.VMEM((levels, cells, meridional.shape[1]), jnp.float32),
    ]
    if pair:
        det = detours(levels, rows, step)
        nd = max(len(d) for d in det)
        dims = (levels, rows, cells, width, n_lon, n_lat, step, det)
        long = pack_room(rows, cells, n_lon, n_lat)
        pack = pltpu.VMEM((2, levels, long, width), jnp.float32)
        few = pltpu.VMEM((2, levels * SUB, width), jnp.float32)
        body = paired
        scratch += [
            pltpu.VMEM((2, nd, step, cells, width), jnp.float32),
            pack,
            pack,
            few,
            few,
            dma((2 * nq + 4,)),
            dma((2, nq, 3)),
            dma((2, nq, 3)),
            dma((2, 2)),
            dma((2, 2)),
            dma((2, nd, 2)),
            dma((2, nd, 2)),
            dma((2, levels + 1)),
            dma((2, levels + 1)),
        ]
    else:
        dims = (levels, rows, cells, width, n_lon, n_lat, step)
        body = general
        scratch += [
            dma((2 * nq + 4,)),
            dma((2, nq, 2 * n_x)),
            dma((2, nq, 2 * n_x)),
            dma((2, 2)),
            dma((2, 2)),
        ]
    vmem = pl.BlockSpec(memory_space=pltpu.VMEM)
    far = pl.BlockSpec(memory_space=pltpu.HBM)
    kept = pltpu.VMEM(tracers.shape, jnp.float32)
    staged = pl.pallas_call(
        functools.partial(body, dims),
        out_shape=(kept, kept),
        in_specs=[far] * 5,
        out_specs=(vmem, vmem),
        scratch_shapes=scratch,
        compiler_params=pltpu.CompilerParams(
            collective_id=0, has_side_effects=True, vmem_limit_bytes=60 << 20
        ),
    )(tracers, adjoint_in, shifts, fractions, jnp.swapaxes(meridional, 1, 2))
    final = jax.ShapeDtypeStruct(tracers.shape, jnp.float32)
    return pl.pallas_call(
        store,
        out_shape=(final, final),
        in_specs=[vmem, vmem],
        out_specs=(far, far),
        scratch_shapes=[dma((2,))],
        compiler_params=pltpu.CompilerParams(vmem_limit_bytes=4 << 20),
    )(*staged)


def solution(mesh):
    block = P("grp", "lat", "lon", None)
    in_specs = (block, block, P(), P(), P(None, None, "lon"))
    return jax.shard_map(
        local, mesh=mesh, in_specs=in_specs, out_specs=(block, block), check_vma=False
    )
```

profile of v0, /device:TPU:0, one launch (start us, length us, event | category | flops | bytes accessed | tf_op | source)
XLA Modules:
  0.0 38.7 jit_solution(7525103205337207583)
XLA Ops:
  0.6 37.0 %shard_map.68 = (f32[2,16,32,128]{3,2,1,0:T(8,128)S(1)}, f32[2,16,32,128]{3,2,1,0:T(8,128)S(1)}) custom-call(f32[2,16,32,128]{3,2,1,0:T(8,128)} %refs_0_.1, f32[2,16,32,128]{3,2,1,0:T(8,128)} %refs_1_.1, s32[2,64]{1,0:T(2,128)} %refs_2_.1, f32[2,64]{1,0:T(2,128)} %refs_3_.1, f32[2,32,64]{2,1,0:T(8,128)} %bitcast.1), custom_call_target="tpu_custom_call" | custom-call | tf_op jit(solution)/shard_map/pallas_call | solution.py:938
  37.7 1.0 %shard_map.69 = (f32[2,16,32,128]{3,2,1,0:T(8,128)}, f32[2,16,32,128]{3,2,1,0:T(8,128)}) custom-call(f32[2,16,32,128]{3,2,1,0:T(8,128)S(1)} %get-tuple-element.4.f_in, f32[2,16,32,128]{3,2,1,0:T(8,128)S(1)} %get-tuple-element.5.a_in), custom_call_target="tpu_custom_call" | custom-call | tf_op jit(solution)/shard_map/pallas_call | solution.py:949
where the time goes:
time: 38.8 us; the launch traced here: 38.7 us
  Pallas kernels  38 us (98%)
  between operations  0.64 us (2%)
    pallas_call x1, Pallas kernels, local(): pl.pallas_call(functools.partial(body, dims), out_shape=(kept, kept), in_...  37 us
    pallas_call x1, Pallas kernels, local(): pl.pallas_call(store, out_shape=(final, final), in_specs=[vmem, vmem], ou...  0.99 us

commit v1 on v0

--- a/solution.py
+++ b/solution.py
@@ -10,6 +10,9 @@
 MESH = pl.DeviceIdType.MESH
 SUB = 8
 RIM = 3
+LAG = 2
+LATE = 4
+HEAD, TAIL = 0, 1
 
 
 def chunk_list(levels, rows, step):
@@ -360,9 +363,6 @@
             gather_drain(a, q)
 
 
-HEAD, TAIL = 0, 1
-
-
 def fits(rows, cells, n_lon, n_lat):
     if n_lon != 4 or n_lat != 4 or rows % 4 or cells % SUB:
         return False
@@ -371,7 +371,7 @@
 
 def detours(levels, rows, step):
     per = rows // step
-    return ((1, 2, per + 2), (1, 2, per + 2))
+    return ((), (1, 2, 3, per + 1, per + 2, per + 3))
 
 
 def pack_plan(rows, cells, n_lon, n_lat, a, side):
@@ -686,7 +686,7 @@
     lanes = lax.broadcasted_iota(jnp.int32, (cells, total_rows), 1)
     for lv in range(levels):
 
-        @pl.loop(0, faces)
+        @pl.loop(0, faces, unroll=faces)
         def _(f):
             row = first + f - 2
             chosen = jnp.logical_and(lanes == row, lanes > 0)
@@ -775,13 +775,21 @@
         far_recv(a, q).wait_recv()
         core_copy(a, q, 1).start()
 
-    def polar_finish(a):
+    def polar_steps(a):
         order = [q for q in range(nq) if q not in det[a]] + list(det[a])
-        for i, q in enumerate(order):
-            relay(a, q)
-            if i > 0:
-                finish(a, order[i - 1])
-        finish(a, order[-1])
+        steps = []
+        for i in range(nq + LAG):
+            if i < nq:
+                steps.append((relay, a, order[i]))
+            if i >= LAG:
+                steps.append((finish, a, order[i - LAG]))
+        return steps
+
+    def polar_run(steps):
+        @pl.when(polar)
+        def _():
+            for act, a, q in steps:
+                act(a, q)
 
     def middle_finish(a):
         for lv in range(levels):
@@ -796,9 +804,7 @@
     for b in dup:
         b.wait()
 
-    @pl.when(polar)
-    def _():
-        polar_finish(0)
+    polar_run(polar_steps(0))
 
     @pl.when(middle)
     def _():
@@ -808,11 +814,13 @@
 
     @pl.when(middle)
     def _():
-        for q in det[0]:
-            pass_on(0, q)
+        for a in range(2):
+            for q in det[a]:
+                pass_on(a, q)
         middle_finish(1)
-        for q in det[1]:
-            pass_on(1, q)
+
+    late = polar_steps(1)
+    polar_run(late[:-LATE])
 
     lat_wait(zb, 1)
 
@@ -842,9 +850,7 @@
                 if u >= 1:
                     of[lv, u - 1, at, :] = z[u - 1] - flux[u] + flux[u - 1]
 
-    @pl.when(polar)
-    def _():
-        polar_finish(1)
+    polar_run(late[-LATE:])
 
     for a in range(2):
         for q in range(nq):

time: 38.8 us -> 26.3 us (0.68)
  Pallas kernels: 38 us -> 25.5 us
    pallas_call x1, Pallas kernels: 37 us -> 24.5 us  [local(): pl.pallas_call(functools.partial(body, dims), out_shape=(kept, kept), in_...]
where the time goes in v1:
time: 26.3 us; the launch traced here: 26.1 us
  Pallas kernels  25.5 us (97%)
  between operations  0.64 us (2%)
    pallas_call x1, Pallas kernels, local(): pl.pallas_call(functools.partial(body, dims), out_shape=(kept, kept), in_...  24.5 us
    pallas_call x1, Pallas kernels, local(): pl.pallas_call(store, out_shape=(final, final), in_specs=[vmem, vmem], ou...  0.99 us

profile of v1, /device:TPU:0, one launch (start us, length us, event | category | flops | bytes accessed | tf_op | source)
XLA Modules:
  0.0 26.1 jit_solution(7423216257124748610)
XLA Ops:
  0.6 24.5 %shard_map.68 = (f32[2,16,32,128]{3,2,1,0:T(8,128)S(1)}, f32[2,16,32,128]{3,2,1,0:T(8,128)S(1)}) custom-call(f32[2,16,32,128]{3,2,1,0:T(8,128)} %refs_0_.1, f32[2,16,32,128]{3,2,1,0:T(8,128)} %refs_1_.1, s32[2,64]{1,0:T(2,128)} %refs_2_.1, f32[2,64]{1,0:T(2,128)} %refs_3_.1, f32[2,32,64]{2,1,0:T(8,128)} %bitcast.1), custom_call_target="tpu_custom_call" | custom-call | tf_op jit(solution)/shard_map/pallas_call | solution.py:944
  25.1 1.0 %shard_map.69 = (f32[2,16,32,128]{3,2,1,0:T(8,128)}, f32[2,16,32,128]{3,2,1,0:T(8,128)}) custom-call(f32[2,16,32,128]{3,2,1,0:T(8,128)S(1)} %get-tuple-element.4.f_in, f32[2,16,32,128]{3,2,1,0:T(8,128)S(1)} %get-tuple-element.5.a_in), custom_call_target="tpu_custom_call" | custom-call | tf_op jit(solution)/shard_map/pallas_call | solution.py:955

commit v2 on v1

--- a/solution.py
+++ b/solution.py
@@ -12,6 +12,9 @@
 RIM = 3
 LAG = 2
 LATE = 4
+HALVES = 2
+SLOW = 2.4
+DETOUR = ((0, 0), (0, 1), (1, 0), (1, 1))
 HEAD, TAIL = 0, 1
 
 
@@ -363,25 +366,22 @@
             gather_drain(a, q)
 
 
-def fits(rows, cells, n_lon, n_lat):
-    if n_lon != 4 or n_lat != 4 or rows % 4 or cells % SUB:
+def reaches(rows, cells, n_lon, n_lat, lat):
+    return [reach(cells * n_lon, rows * n_lat, lat * rows + k) + RIM for k in range(rows)]
+
+
+def fits(levels, rows, cells, n_lon, n_lat):
+    if levels != 2 or n_lon != 4 or n_lat != 4 or rows % 8 or cells % SUB:
         return False
-    return reach(cells * n_lon, rows * n_lat, rows) + RIM <= cells + SUB
-
-
-def detours(levels, rows, step):
-    per = rows // step
-    return ((), (1, 2, 3, per + 1, per + 2, per + 3))
-
-
-def pack_plan(rows, cells, n_lon, n_lat, a, side):
-    big = (side == TAIL) == (a == 0)
+    outer = reaches(rows, cells, n_lon, n_lat, 0)[-(rows // 4) :]
+    inner = reaches(rows, cells, n_lon, n_lat, 1)
+    return cells < min(outer) and max(outer) <= 2 * cells and max(inner) <= cells + SUB
+
+
+def plan_of(cells, sizes, side):
     slots = []
     at = SUB
-    for k in range(rows):
-        s = RIM - 1
-        if big:
-            s = min(reach(cells * n_lon, rows * n_lat, rows + k) + RIM, cells)
+    for s in sizes:
         if s >= SUB:
             begins = list(range(0, s - SUB + 1, SUB))
             if s % SUB:
@@ -393,8 +393,21 @@
         else:
             slots.append([(0, at)])
         at += s
-    long = -(-(at - SUB) // SUB) * SUB
-    return slots, long
+    return slots, -(-(at - SUB) // SUB) * SUB
+
+
+def pack_plan(rows, cells, n_lon, n_lat, a, side):
+    sizes = [RIM - 1] * rows
+    if (side == TAIL) == (a == 0):
+        sizes = [min(m, cells) for m in reaches(rows, cells, n_lon, n_lat, 1)]
+    return plan_of(cells, sizes, side)
+
+
+def trim_plan(rows, cells, n_lon, n_lat, a):
+    step = rows // 4
+    sizes = [m - cells for m in reaches(rows, cells, n_lon, n_lat, 0)[-step:]]
+    near = TAIL if a == 0 else HEAD
+    return near, plan_of(cells, sizes, near), plan_of(cells, [RIM - 1] * step, 1 - near)
 
 
 def pack_room(rows, cells, n_lon, n_lat):
@@ -403,15 +416,21 @@
     )
 
 
+def trim_room(rows, cells, n_lon, n_lat):
+    return 2 * SUB + max(
+        plan[1] for a in range(2) for plan in trim_plan(rows, cells, n_lon, n_lat, a)[1:]
+    )
+
+
 def paired(dims, *refs):
-    levels, rows, cells, width, n_lon, n_lat, step, det = dims
+    levels, rows, cells, width, n_lon, n_lat, step = dims
     chunks = chunk_list(levels, rows, step)
     nq = len(chunks)
     per = rows // step
     tr, ad, shifts_in, fractions_in, mer_in, of, oa = refs[:7]
     gath = (refs[7 : 7 + nq], refs[7 + nq : 7 + 2 * nq])
     zb, ab, vb, taps, shifts, fractions, mer, held = refs[7 + 2 * nq : 15 + 2 * nq]
-    sendp, recvp, sendx, recvx, loc, ssem, rsem, hs, hr, vs, vr, ps, pr = refs[15 + 2 * nq :]
+    sendp, recvp, sendx, recvx, loc, ssem, rsem, hs, hr, vs, vr, ps, pr, sendt, recvt, ts, tr_, ready = refs[15 + 2 * nq :]
     total_cells = cells * n_lon
     total_rows = rows * n_lat
 
@@ -425,6 +444,23 @@
     mate = lat + 1 - 2 * lax.rem(lat, 2)
     middle = jnp.logical_and(lat > 0, lat < n_lat - 1)
     polar = jnp.logical_not(middle)
+
+    barrier = pltpu.get_barrier_semaphore()
+
+    def greet(**place):
+        pl.semaphore_signal(barrier, inc=1, device_id=place, device_id_type=MESH)
+
+    greet(lon=partner)
+    greet(lon=beside)
+    greet(lon=joint)
+
+    @pl.when(lat > 0)
+    def _():
+        greet(lat=lat - 1)
+
+    @pl.when(lat < n_lat - 1)
+    def _():
+        greet(lat=lat + 1)
 
     own = []
     dup = []
@@ -452,27 +488,10 @@
         b.start()
         dup.append(b)
 
-    barrier = pltpu.get_barrier_semaphore()
-
-    def greet(**place):
-        pl.semaphore_signal(barrier, inc=1, device_id=place, device_id_type=MESH)
-
-    greet(lon=partner)
-    greet(lon=beside)
-    greet(lon=beside, lat=mate)
-
-    @pl.when(lat > 0)
-    def _():
-        greet(lat=lat - 1)
-
-    @pl.when(lat < n_lat - 1)
-    def _():
-        greet(lat=lat + 1)
-
     @pl.when(middle)
     def _():
-        greet(lon=joint)
-        pl.semaphore_wait(barrier, 6)
+        pl.semaphore_wait(barrier, 5)
+        pl.semaphore_signal(ready, inc=1, device_id={"lat": mate}, device_id_type=MESH)
 
     @pl.when(polar)
     def _():
@@ -483,21 +502,25 @@
             source, target, send, recv, device_id=place, device_id_type=MESH
         )
 
-    def lat_copies(buf, k):
+    def lat_copies(buf, k, lv):
         down = remote(
-            buf.at[:, pl.ds(RIM, RIM)],
-            buf.at[:, pl.ds(RIM + rows, RIM)],
-            hs.at[k, 0],
-            hr.at[k, 0],
+            buf.at[lv, pl.ds(RIM, RIM)],
+            buf.at[lv, pl.ds(RIM + rows, RIM)],
+            hs.at[k, lv, 0],
+            hr.at[k, lv, 0],
             lat=lat - 1,
         )
         up = remote(
-            buf.at[:, pl.ds(rows, RIM)], buf.at[:, pl.ds(0, RIM)], hs.at[k, 1], hr.at[k, 1], lat=lat + 1
+            buf.at[lv, pl.ds(rows, RIM)],
+            buf.at[lv, pl.ds(0, RIM)],
+            hs.at[k, lv, 1],
+            hr.at[k, lv, 1],
+            lat=lat + 1,
         )
         return down, up
 
-    def lat_start(buf, k):
-        down, up = lat_copies(buf, k)
+    def lat_start(buf, k, lv):
+        down, up = lat_copies(buf, k, lv)
 
         @pl.when(lat > 0)
         def _():
@@ -507,8 +530,8 @@
         def _():
             up.start()
 
-    def lat_wait(buf, k):
-        down, up = lat_copies(buf, k)
+    def lat_wait(buf, k, lv):
+        down, up = lat_copies(buf, k, lv)
 
         @pl.when(lat > 0)
         def _():
@@ -541,29 +564,50 @@
             lon=partner,
         )
 
-    def out_copy(a, q):
-        i = det[a].index(q)
+    piece = step // HALVES
+
+    def chunk_at(lv, k, south):
+        return lv * per + (k if south else per - 1 - k)
+
+    def polar_half(act):
+        for south in (True, False):
+
+            @pl.when(lat == (0 if south else n_lat - 1))
+            def _():
+                act(south)
+
+    def out_copy(i, h, south):
+        q = chunk_at(*DETOUR[i], south)
         return remote(
-            gath[a][q].at[:, own_block],
-            held.at[a, i],
-            vs.at[a, i, 0],
-            vr.at[a, i, 0],
+            gath[1][q].at[pl.ds(h * piece, piece), own_block],
+            held.at[i, pl.ds(h * piece, piece)],
+            vs.at[i, h, 0],
+            vr.at[i, h, 0],
             lon=beside,
             lat=mate,
         )
 
-    def on_copy(a, q):
-        i = det[a].index(q)
+    def on_copy(i, h, south):
+        q = chunk_at(*DETOUR[i], south)
         return remote(
-            held.at[a, i], gath[a][q].at[:, far_block], vs.at[a, i, 1], vr.at[a, i, 1], lat=mate
-        )
-
-    def far_send(a, q):
-        return out_copy(a, q) if q in det[a] else x_copy(a, q)
-
-    def far_recv(a, q):
-        return on_copy(a, q) if q in det[a] else x_copy(a, q)
-
+            held.at[i, pl.ds(h * piece, piece)],
+            gath[1][q].at[pl.ds(h * piece, piece), far_block],
+            vs.at[i, h, 1],
+            vr.at[i, h, 1],
+            lat=mate,
+        )
+
+    def trim_copy(a, lv, w):
+        long = trims[a][1 + w][1]
+        return remote(
+            sendt.at[a, lv, w, pl.ds(SUB, long)],
+            recvt.at[a, lv, w, pl.ds(SUB, long)],
+            ts.at[a, lv, w],
+            tr_.at[a, lv, w],
+            lon=joint if w else beside,
+        )
+
+    trims = [trim_plan(rows, cells, n_lon, n_lat, a) for a in range(2)]
     plans = [[pack_plan(rows, cells, n_lon, n_lat, a, side) for side in (HEAD, TAIL)] for a in range(2)]
     ring = (cells, (n_lon - 1) * cells)
     spill = [
@@ -647,24 +691,109 @@
 
             by_half(few)
 
-    def pass_on(a, q):
-        out_copy(a, q).wait_recv()
-        on_copy(a, q).start()
+    def trim_send(a, lv, south):
+        near, *pair = trims[a]
+        for w in range(2):
+            side = 1 - near if w else near
+            slots = pair[w][0]
+            order = range(step) if side == HEAD else reversed(range(step))
+            for k in order:
+                q, j = place_of(lv, rows - step + k, south)
+                for source, target in slots[k]:
+                    sendt[a, lv, w, pl.ds(target, SUB), :] = gath[a][q][j, pl.ds(source, SUB), :]
+            trim_copy(a, lv, w).start()
+
+    def trim_take(a, lv, w, south):
+        near, *pair = trims[a]
+        base = ring[1 - near] if w else 2 * cells
+        trim_copy(a, lv, w).wait_recv()
+        for k in range(step):
+            q, j = place_of(lv, rows - step + k, south)
+            for source, target in pair[w][0][k]:
+                gath[a][q][j, pl.ds(base + source, SUB), :] = recvt[a, lv, w, pl.ds(target, SUB), :]
+
+    def kind(a, lv, k):
+        if k == per - 1:
+            return "trim"
+        return "detour" if a == 1 and (lv, k) in DETOUR else "direct"
+
+    def far_send(a, lv, k, south):
+        q = chunk_at(lv, k, south)
+        if kind(a, lv, k) == "detour":
+            for h in range(HALVES):
+                out_copy(DETOUR.index((lv, k)), h, south).start()
+        elif kind(a, lv, k) == "direct":
+            x_copy(a, q).start()
+        else:
+
+            @pl.when(core == 1 - a)
+            def _():
+                x_copy(a, q).start()
+
+            @pl.when(core == a)
+            def _():
+                trim_send(a, lv, south)
+
+    def relay(a, lv, k, south):
+        q = chunk_at(lv, k, south)
+        if kind(a, lv, k) == "detour":
+            for h in range(HALVES):
+                on_copy(DETOUR.index((lv, k)), h, south).wait_recv()
+            core_copy(a, q, 1).start()
+        elif kind(a, lv, k) == "direct":
+            x_copy(a, q).wait_recv()
+            core_copy(a, q, 1).start()
+        else:
+
+            @pl.when(core == 1 - a)
+            def _():
+                x_copy(a, q).wait_recv()
+                core_copy(a, q, 1).start()
+                trim_take(a, lv, 1, south)
+
+            @pl.when(core == a)
+            def _():
+                trim_take(a, lv, 0, south)
+
+    def far_done(a, lv, k, south):
+        q = chunk_at(lv, k, south)
+        if kind(a, lv, k) == "detour":
+            for h in range(HALVES):
+                out_copy(DETOUR.index((lv, k)), h, south).wait_send()
+            core_copy(a, q, 1).wait_send()
+        elif kind(a, lv, k) == "direct":
+            x_copy(a, q).wait_send()
+            core_copy(a, q, 1).wait_send()
+        else:
+
+            @pl.when(core == 1 - a)
+            def _():
+                x_copy(a, q).wait_send()
+                core_copy(a, q, 1).wait_send()
+
+            @pl.when(core == a)
+            def _():
+                for w in range(2):
+                    trim_copy(a, lv, w).wait_send()
+
+    def pass_on(south):
+        for i in range(len(DETOUR)):
+            for h in range(HALVES):
+                out_copy(i, h, south).wait_recv()
+                on_copy(i, h, south).start()
 
     def send_level(a, lv):
-        for q in range(lv * per, (lv + 1) * per):
-            core_copy(a, q, 0).start()
-
-            @pl.when(polar)
-            def _():
-                far_send(a, q).start()
+        polar_half(lambda south: [far_send(a, lv, k, south) for k in range(per)])
 
         @pl.when(middle)
         def _():
             pack_send(a, lv)
 
+        for q in range(lv * per, (lv + 1) * per):
+            core_copy(a, q, 0).start()
+
     adc.wait()
-    lat_start(ab, 0)
+    lat_start(ab, 0, 0)
     for lv in range(levels):
         for q in range(lv * per, (lv + 1) * per):
             own[q].wait()
@@ -693,13 +822,16 @@
             column = jnp.sum(jnp.where(chosen, mer[lv], 0.0), axis=1, keepdims=True)
             vb[lv, f] = jnp.broadcast_to(column, (cells, width))
 
+        if lv + 1 < levels:
+            lat_start(ab, 0, lv + 1)
+
         @pl.loop(0, rows)
         def _(r):
             for k, t in enumerate(zonal_taps(fractions[lv, first + r])):
                 taps[(lv * rows + r) * 6 + k] = t
 
-    lat_wait(ab, 0)
     for lv in range(levels):
+        lat_wait(ab, 0, lv)
 
         @pl.loop(0, cells // SUB)
         def _(c):
@@ -738,6 +870,12 @@
                         r % step, pl.ds(pl.multiple_of(total_cells + c * SUB, SUB), SUB), :
                     ] = value
 
+        if lv == 0:
+
+            @pl.when(polar)
+            def _():
+                pl.semaphore_wait(ready, 1)
+
         send_level(1, lv)
 
     def sweep(a, q, sink, sink_row, sign):
@@ -763,33 +901,38 @@
                     total = term if total is None else total + term
                 sink[lv, sink_row + r0 + r, pl.ds(c * SUB, SUB), :] = total
 
-    def finish(a, q):
-        for dx in range(2):
-            core_copy(a, q, dx).wait_recv()
+    def finish(a, lv, k, south):
+        q = chunk_at(lv, k, south)
+        core_copy(a, q, 0).wait_recv()
+        if kind(a, lv, k) == "trim":
+
+            @pl.when(core == a)
+            def _():
+                core_copy(a, q, 1).wait_recv()
+
+        else:
+            core_copy(a, q, 1).wait_recv()
         if a == 0:
             sweep(0, q, zb, RIM, -1)
         else:
             sweep(1, q, oa, 0, 1)
 
-    def relay(a, q):
-        far_recv(a, q).wait_recv()
-        core_copy(a, q, 1).start()
-
     def polar_steps(a):
-        order = [q for q in range(nq) if q not in det[a]] + list(det[a])
+        spots = [(lv, k) for lv in range(levels) for k in range(per)]
+        direct = [p for p in spots if kind(a, *p) != "detour"]
+        due = {p: i + SLOW for i, p in enumerate(direct)}
+        due.update({p: i for i, p in enumerate(DETOUR) if a == 1})
+        order = sorted(spots, key=lambda p: due[p])
         steps = []
         for i in range(nq + LAG):
             if i < nq:
-                steps.append((relay, a, order[i]))
+                steps.append((relay, a) + order[i])
             if i >= LAG:
-                steps.append((finish, a, order[i - LAG]))
+                steps.append((finish, a) + order[i - LAG])
         return steps
 
     def polar_run(steps):
-        @pl.when(polar)
-        def _():
-            for act, a, q in steps:
-                act(a, q)
+        polar_half(lambda south: [step_[0](*step_[1:], south) for step_ in steps])
 
     def middle_finish(a):
         for lv in range(levels):
@@ -810,21 +953,19 @@
     def _():
         middle_finish(0)
 
-    lat_start(zb, 1)
+    for lv in range(levels):
+        lat_start(zb, 1, lv)
 
     @pl.when(middle)
     def _():
-        for a in range(2):
-            for q in det[a]:
-                pass_on(a, q)
+        by_half(pass_on)
         middle_finish(1)
 
     late = polar_steps(1)
     polar_run(late[:-LATE])
 
-    lat_wait(zb, 1)
-
     for lv in range(levels):
+        lat_wait(zb, 1, lv)
 
         @pl.loop(0, cells // SUB)
         def _(c):
@@ -855,16 +996,21 @@
     for a in range(2):
         for q in range(nq):
             core_copy(a, q, 0).wait_send()
-
-            @pl.when(polar)
-            def _():
-                far_send(a, q).wait_send()
-                core_copy(a, q, 1).wait_send()
-
-        @pl.when(middle)
-        def _():
-            for q in det[a]:
-                on_copy(a, q).wait_send()
+    polar_half(
+        lambda south: [
+            far_done(a, lv, k, south) for a in range(2) for lv in range(levels) for k in range(per)
+        ]
+    )
+
+    @pl.when(middle)
+    def _():
+        def sent(south):
+            for i in range(len(DETOUR)):
+                for h in range(HALVES):
+                    on_copy(i, h, south).wait_send()
+
+        by_half(sent)
+        for a in range(2):
             for lv in range(levels):
                 for side in (HEAD, TAIL):
 
@@ -889,7 +1035,7 @@
     levels, rows, cells, width = tracers.shape
     n_lon, n_lat = lax.axis_size("lon"), lax.axis_size("lat")
     n_x = n_lon // 2
-    pair = fits(rows, cells, n_lon, n_lat)
+    pair = fits(levels, rows, cells, n_lon, n_lat)
     step = max(1, rows // (4 if pair else 2))
     nq = levels * (rows // step)
     dma = pltpu.SemaphoreType.DMA
@@ -905,15 +1051,17 @@
         pltpu.VMEM((levels, cells, meridional.shape[1]), jnp.float32),
     ]
     if pair:
-        det = detours(levels, rows, step)
-        nd = max(len(d) for d in det)
-        dims = (levels, rows, cells, width, n_lon, n_lat, step, det)
+        nd = len(DETOUR)
+        dims = (levels, rows, cells, width, n_lon, n_lat, step)
         long = pack_room(rows, cells, n_lon, n_lat)
         pack = pltpu.VMEM((2, levels, long, width), jnp.float32)
+        trim = pltpu.VMEM(
+            (2, levels, 2, trim_room(rows, cells, n_lon, n_lat), width), jnp.float32
+        )
         few = pltpu.VMEM((2, levels * SUB, width), jnp.float32)
         body = paired
         scratch += [
-            pltpu.VMEM((2, nd, step, cells, width), jnp.float32),
+            pltpu.VMEM((nd, step, cells, width), jnp.float32),
             pack,
             pack,
             few,
@@ -921,12 +1069,17 @@
             dma((2 * nq + 4,)),
             dma((2, nq, 3)),
             dma((2, nq, 3)),
-            dma((2, 2)),
-            dma((2, 2)),
-            dma((2, nd, 2)),
-            dma((2, nd, 2)),
+            dma((2, levels, 2)),
+            dma((2, levels, 2)),
+            dma((nd, HALVES, 2)),
+            dma((nd, HALVES, 2)),
             dma((2, levels + 1)),
             dma((2, levels + 1)),
+            trim,
+            trim,
+            dma((2, levels, 2)),
+            dma((2, levels, 2)),
+            pltpu.SemaphoreType.REGULAR,
         ]
     else:
         dims = (levels, rows, cells, width, n_lon, n_lat, step)

time: 26.3 us -> 24.8 us (0.943)
  Pallas kernels: 25.5 us -> 23.9 us
    pallas_call x1, Pallas kernels: 24.5 us -> 23 us  [local(): pl.pallas_call(functools.partial(body, dims), out_shape=(kept, kept), in_...]
where the time goes in v2:
time: 24.8 us; the launch traced here: 24.6 us
  Pallas kernels  23.9 us (96%)
  between operations  0.64 us (3%)
    pallas_call x1, Pallas kernels, local(): pl.pallas_call(functools.partial(body, dims), out_shape=(kept, kept), in_...  23 us
    pallas_call x1, Pallas kernels, local(): pl.pallas_call(store, out_shape=(final, final), in_specs=[vmem, vmem], ou...  0.99 us

profile of v2, /device:TPU:0, one launch (start us, length us, event | category | flops | bytes accessed | tf_op | source)
XLA Modules:
  0.0 24.6 jit_solution(10170567299590134239)
XLA Ops:
  0.6 23.0 %shard_map.68 = (f32[2,16,32,128]{3,2,1,0:T(8,128)S(1)}, f32[2,16,32,128]{3,2,1,0:T(8,128)S(1)}) custom-call(f32[2,16,32,128]{3,2,1,0:T(8,128)} %refs_0_.1, f32[2,16,32,128]{3,2,1,0:T(8,128)} %refs_1_.1, s32[2,64]{1,0:T(2,128)} %refs_2_.1, f32[2,64]{1,0:T(2,128)} %refs_3_.1, f32[2,32,64]{2,1,0:T(8,128)} %bitcast.1), custom_call_target="tpu_custom_call" | custom-call | tf_op jit(solution)/shard_map/pallas_call | solution.py:1097
  23.6 1.0 %shard_map.69 = (f32[2,16,32,128]{3,2,1,0:T(8,128)}, f32[2,16,32,128]{3,2,1,0:T(8,128)}) custom-call(f32[2,16,32,128]{3,2,1,0:T(8,128)S(1)} %get-tuple-element.4.f_in, f32[2,16,32,128]{3,2,1,0:T(8,128)S(1)} %get-tuple-element.5.a_in), custom_call_target="tpu_custom_call" | custom-call | tf_op jit(solution)/shard_map/pallas_call | solution.py:1108

commit v3 on v2

--- a/solution.py
+++ b/solution.py
@@ -430,7 +430,8 @@
     tr, ad, shifts_in, fractions_in, mer_in, of, oa = refs[:7]
     gath = (refs[7 : 7 + nq], refs[7 + nq : 7 + 2 * nq])
     zb, ab, vb, taps, shifts, fractions, mer, held = refs[7 + 2 * nq : 15 + 2 * nq]
-    sendp, recvp, sendx, recvx, loc, ssem, rsem, hs, hr, vs, vr, ps, pr, sendt, recvt, ts, tr_, ready = refs[15 + 2 * nq :]
+    sendp, recvp, sendx, recvx, sendt, recvt = refs[15 + 2 * nq : 21 + 2 * nq]
+    loc, sx, sc, sd, st, sh, rf, rc0, rc1, rt, rh, ready = refs[21 + 2 * nq :]
     total_cells = cells * n_lon
     total_rows = rows * n_lat
 
@@ -462,31 +463,30 @@
     def _():
         greet(lat=lat + 1)
 
-    own = []
-    dup = []
+    def take(ref, sem):
+        pltpu.make_async_copy(ref, ref, sem).wait()
+
+    def lump(m):
+        return tr.at[:, pl.ds(0, m * step // levels)]
+
     for q, (lv, r0) in enumerate(chunks):
-        a = pltpu.make_async_copy(
-            tr.at[lv, pl.ds(r0, step)], gath[0][q].at[:, pl.ds(0, cells)], loc.at[q]
-        )
-        a.start()
-        own.append(a)
-    adc = pltpu.make_async_copy(ad, ab.at[:, pl.ds(RIM, rows)], loc.at[2 * nq])
-    adc.start()
+        pltpu.make_async_copy(
+            tr.at[lv, pl.ds(r0, step)], gath[0][q].at[:, pl.ds(0, cells)], loc.at[lv]
+        ).start()
+    pltpu.make_async_copy(ad, ab.at[:, pl.ds(RIM, rows)], loc.at[levels]).start()
     small = []
     for k, (source, target) in enumerate(
         ((shifts_in, shifts), (fractions_in, fractions), (mer_in, mer))
     ):
-        d = pltpu.make_async_copy(source, target, loc.at[2 * nq + 1 + k])
+        d = pltpu.make_async_copy(source, target, loc.at[levels + 2 + k])
         d.start()
         small.append(d)
     for q, (lv, r0) in enumerate(chunks):
-        b = pltpu.make_async_copy(
+        pltpu.make_async_copy(
             tr.at[lv, pl.ds(r0, step)],
             gath[0][q].at[:, pl.ds(total_cells, cells)],
-            loc.at[nq + q],
-        )
-        b.start()
-        dup.append(b)
+            loc.at[levels + 1],
+        ).start()
 
     @pl.when(middle)
     def _():
@@ -506,15 +506,15 @@
         down = remote(
             buf.at[lv, pl.ds(RIM, RIM)],
             buf.at[lv, pl.ds(RIM + rows, RIM)],
-            hs.at[k, lv, 0],
-            hr.at[k, lv, 0],
+            sh.at[k, 0],
+            rh.at[k, lv],
             lat=lat - 1,
         )
         up = remote(
             buf.at[lv, pl.ds(rows, RIM)],
             buf.at[lv, pl.ds(0, RIM)],
-            hs.at[k, lv, 1],
-            hr.at[k, lv, 1],
+            sh.at[k, 1],
+            rh.at[k, lv],
             lat=lat + 1,
         )
         return down, up
@@ -530,18 +530,14 @@
         def _():
             up.start()
 
-    def lat_wait(buf, k, lv):
-        down, up = lat_copies(buf, k, lv)
-
-        @pl.when(lat > 0)
-        def _():
-            down.wait_send()
-            up.wait_recv()
-
-        @pl.when(lat < n_lat - 1)
-        def _():
-            up.wait_send()
-            down.wait_recv()
+    def lat_wait(k, lv):
+        @pl.when(polar)
+        def _():
+            take(tr.at[lv, pl.ds(0, RIM)], rh.at[k, lv])
+
+        @pl.when(middle)
+        def _():
+            take(tr.at[lv, pl.ds(0, 2 * RIM)], rh.at[k, lv])
 
     own_block = pl.ds(0, cells)
     far_block = pl.ds((n_lon - 2) * cells, cells)
@@ -549,7 +545,7 @@
     def x_copy(a, q):
         g = gath[a][q]
         return remote(
-            g.at[:, own_block], g.at[:, far_block], ssem.at[a, q, 0], rsem.at[a, q, 0], lon=beside
+            g.at[:, own_block], g.at[:, far_block], sx.at[a], rf.at[a, q], lon=beside
         )
 
     def core_copy(a, q, dx):
@@ -559,8 +555,8 @@
         return remote(
             g.at[:, pl.ds(source, cells)],
             g.at[:, pl.ds(pl.multiple_of(slot * cells, SUB), cells)],
-            ssem.at[a, q, 1 + dx],
-            rsem.at[a, q, 1 + dx],
+            sc.at[a, dx],
+            rc1.at[a, q] if dx else rc0.at[a, q // per],
             lon=partner,
         )
 
@@ -581,8 +577,8 @@
         return remote(
             gath[1][q].at[pl.ds(h * piece, piece), own_block],
             held.at[i, pl.ds(h * piece, piece)],
-            vs.at[i, h, 0],
-            vr.at[i, h, 0],
+            sd.at[0],
+            rf.at[(i * HALVES + h) // nq, (i * HALVES + h) % nq],
             lon=beside,
             lat=mate,
         )
@@ -592,8 +588,8 @@
         return remote(
             held.at[i, pl.ds(h * piece, piece)],
             gath[1][q].at[pl.ds(h * piece, piece), far_block],
-            vs.at[i, h, 1],
-            vr.at[i, h, 1],
+            sd.at[0],
+            rf.at[1, q],
             lat=mate,
         )
 
@@ -602,8 +598,8 @@
         return remote(
             sendt.at[a, lv, w, pl.ds(SUB, long)],
             recvt.at[a, lv, w, pl.ds(SUB, long)],
-            ts.at[a, lv, w],
-            tr_.at[a, lv, w],
+            st.at[w],
+            rt.at[a, lv],
             lon=joint if w else beside,
         )
 
@@ -631,13 +627,13 @@
         return remote(
             sendp.at[a, lv, pl.ds(SUB, long)],
             recvp.at[a, lv, pl.ds(SUB, long)],
-            ps.at[a, lv],
-            pr.at[a, lv],
+            sc.at[a, 1],
+            rc1.at[a, lv],
             lon=joint,
         )
 
     def few_copy(a):
-        return remote(sendx.at[a], recvx.at[a], ps.at[a, levels], pr.at[a, levels], lon=beside)
+        return remote(sendx.at[a], recvx.at[a], sx.at[a], rc1.at[a, levels], lon=beside)
 
     def pack_send(a, lv):
         for side in (HEAD, TAIL):
@@ -737,8 +733,7 @@
     def relay(a, lv, k, south):
         q = chunk_at(lv, k, south)
         if kind(a, lv, k) == "detour":
-            for h in range(HALVES):
-                on_copy(DETOUR.index((lv, k)), h, south).wait_recv()
+            take(gath[1][q].at[:, far_block], rf.at[1, q])
             core_copy(a, q, 1).start()
         elif kind(a, lv, k) == "direct":
             x_copy(a, q).wait_recv()
@@ -755,27 +750,6 @@
             def _():
                 trim_take(a, lv, 0, south)
 
-    def far_done(a, lv, k, south):
-        q = chunk_at(lv, k, south)
-        if kind(a, lv, k) == "detour":
-            for h in range(HALVES):
-                out_copy(DETOUR.index((lv, k)), h, south).wait_send()
-            core_copy(a, q, 1).wait_send()
-        elif kind(a, lv, k) == "direct":
-            x_copy(a, q).wait_send()
-            core_copy(a, q, 1).wait_send()
-        else:
-
-            @pl.when(core == 1 - a)
-            def _():
-                x_copy(a, q).wait_send()
-                core_copy(a, q, 1).wait_send()
-
-            @pl.when(core == a)
-            def _():
-                for w in range(2):
-                    trim_copy(a, lv, w).wait_send()
-
     def pass_on(south):
         for i in range(len(DETOUR)):
             for h in range(HALVES):
@@ -792,11 +766,10 @@
         for q in range(lv * per, (lv + 1) * per):
             core_copy(a, q, 0).start()
 
-    adc.wait()
+    take(ad, loc.at[levels])
     lat_start(ab, 0, 0)
     for lv in range(levels):
-        for q in range(lv * per, (lv + 1) * per):
-            own[q].wait()
+        take(tr.at[lv], loc.at[lv])
         send_level(0, lv)
 
     @pl.when(lat == 0)
@@ -831,7 +804,7 @@
                 taps[(lv * rows + r) * 6 + k] = t
 
     for lv in range(levels):
-        lat_wait(ab, 0, lv)
+        lat_wait(0, lv)
 
         @pl.loop(0, cells // SUB)
         def _(c):
@@ -901,9 +874,11 @@
                     total = term if total is None else total + term
                 sink[lv, sink_row + r0 + r, pl.ds(c * SUB, SUB), :] = total
 
+    def level_take(a, lv, k=0, south=True):
+        take(tr.at[lv], rc0.at[a, lv])
+
     def finish(a, lv, k, south):
         q = chunk_at(lv, k, south)
-        core_copy(a, q, 0).wait_recv()
         if kind(a, lv, k) == "trim":
 
             @pl.when(core == a)
@@ -924,11 +899,16 @@
         due.update({p: i for i, p in enumerate(DETOUR) if a == 1})
         order = sorted(spots, key=lambda p: due[p])
         steps = []
+        ready_levels = []
         for i in range(nq + LAG):
             if i < nq:
                 steps.append((relay, a) + order[i])
             if i >= LAG:
-                steps.append((finish, a) + order[i - LAG])
+                lv, k = order[i - LAG]
+                if lv not in ready_levels:
+                    ready_levels.append(lv)
+                    steps.append((level_take, a, lv, k))
+                steps.append((finish, a, lv, k))
         return steps
 
     def polar_run(steps):
@@ -937,15 +917,14 @@
     def middle_finish(a):
         for lv in range(levels):
             pack_take(a, lv)
+            level_take(a, lv)
             for q in range(lv * per, (lv + 1) * per):
-                core_copy(a, q, 0).wait_recv()
                 if a == 0:
                     sweep(0, q, zb, RIM, -1)
                 else:
                     sweep(1, q, oa, 0, 1)
 
-    for b in dup:
-        b.wait()
+    take(tr, loc.at[levels + 1])
 
     polar_run(polar_steps(0))
 
@@ -965,7 +944,7 @@
     polar_run(late[:-LATE])
 
     for lv in range(levels):
-        lat_wait(zb, 1, lv)
+        lat_wait(1, lv)
 
         @pl.loop(0, cells // SUB)
         def _(c):
@@ -993,33 +972,44 @@
 
     polar_run(late[-LATE:])
 
+    take(lump(len(DETOUR)), sd.at[0])
+    for k in range(2):
+
+        @pl.when(lat > 0)
+        def _():
+            take(tr.at[:, pl.ds(0, RIM)], sh.at[k, 0])
+
+        @pl.when(lat < n_lat - 1)
+        def _():
+            take(tr.at[:, pl.ds(0, RIM)], sh.at[k, 1])
+
     for a in range(2):
-        for q in range(nq):
-            core_copy(a, q, 0).wait_send()
-    polar_half(
-        lambda south: [
-            far_done(a, lv, k, south) for a in range(2) for lv in range(levels) for k in range(per)
-        ]
-    )
-
-    @pl.when(middle)
-    def _():
-        def sent(south):
-            for i in range(len(DETOUR)):
-                for h in range(HALVES):
-                    on_copy(i, h, south).wait_send()
-
-        by_half(sent)
-        for a in range(2):
-            for lv in range(levels):
-                for side in (HEAD, TAIL):
-
-                    @pl.when(core == side)
-                    def _():
-                        pack_copy(a, lv, side).wait_send()
-
-            if spill:
-                few_copy(a).wait_send()
+        take(tr, sc.at[a, 0])
+        straight = nq - levels - (len(DETOUR) if a == 1 else 0)
+
+        @pl.when(jnp.logical_and(polar, core == a))
+        def _():
+            take(lump(straight), sx.at[a])
+            take(lump(nq - levels), sc.at[a, 1])
+            for w in range(2):
+                take(sendt.at[a, :, w, pl.ds(SUB, trims[a][1 + w][1])], st.at[w])
+
+        @pl.when(jnp.logical_and(polar, core == 1 - a))
+        def _():
+            take(lump(straight + levels), sx.at[a])
+            take(tr, sc.at[a, 1])
+
+        for side in (HEAD, TAIL):
+
+            @pl.when(jnp.logical_and(middle, core == side))
+            def _():
+                take(sendp.at[a, :, pl.ds(SUB, plans[a][side][1])], sc.at[a, 1])
+
+        if spill:
+
+            @pl.when(middle)
+            def _():
+                take(sendx.at[a], sx.at[a])
 
 
 def store(f_in, a_in, f_out, a_out, sem):
@@ -1066,19 +1056,19 @@
             pack,
             few,
             few,
-            dma((2 * nq + 4,)),
-            dma((2, nq, 3)),
-            dma((2, nq, 3)),
-            dma((2, levels, 2)),
-            dma((2, levels, 2)),
-            dma((nd, HALVES, 2)),
-            dma((nd, HALVES, 2)),
-            dma((2, levels + 1)),
-            dma((2, levels + 1)),
             trim,
             trim,
-            dma((2, levels, 2)),
-            dma((2, levels, 2)),
+            dma((levels + 5,)),
+            dma((2,)),
+            dma((2, 2)),
+            dma((1,)),
+            dma((2,)),
+            dma((2, 2)),
+            dma((2, nq)),
+            dma((2, levels)),
+            dma((2, nq)),
+            dma((2, levels)),
+            dma((2, levels)),
             pltpu.SemaphoreType.REGULAR,
         ]
     else:

time: 24.8 us -> 23.6 us (0.952)
  Pallas kernels: 23.9 us -> 22.8 us
    pallas_call x1, Pallas kernels: 23 us -> 21.8 us  [local(): pl.pallas_call(functools.partial(body, dims), out_shape=(kept, kept), in_...]
where the time goes in v3:
time: 23.6 us; the launch traced here: 23.4 us
  Pallas kernels  22.8 us (97%)
  between operations  0.64 us (3%)
    pallas_call x1, Pallas kernels, local(): pl.pallas_call(functools.partial(body, dims), out_shape=(kept, kept), in_...  21.8 us
    pallas_call x1, Pallas kernels, local(): pl.pallas_call(store, out_shape=(final, final), in_specs=[vmem, vmem], ou...  0.99 us

profile of v3, /device:TPU:0, one launch (start us, length us, event | category | flops | bytes accessed | tf_op | source)
XLA Modules:
  0.0 23.4 jit_solution(10082527154189102332)
XLA Ops:
  0.6 21.8 %shard_map.68 = (f32[2,16,32,128]{3,2,1,0:T(8,128)S(1)}, f32[2,16,32,128]{3,2,1,0:T(8,128)S(1)}) custom-call(f32[2,16,32,128]{3,2,1,0:T(8,128)} %refs_0_.1, f32[2,16,32,128]{3,2,1,0:T(8,128)} %refs_1_.1, s32[2,64]{1,0:T(2,128)} %refs_2_.1, f32[2,64]{1,0:T(2,128)} %refs_3_.1, f32[2,32,64]{2,1,0:T(8,128)} %bitcast.1), custom_call_target="tpu_custom_call" | custom-call | tf_op jit(solution)/shard_map/pallas_call | solution.py:1087
  22.4 1.0 %shard_map.69 = (f32[2,16,32,128]{3,2,1,0:T(8,128)}, f32[2,16,32,128]{3,2,1,0:T(8,128)}) custom-call(f32[2,16,32,128]{3,2,1,0:T(8,128)S(1)} %get-tuple-element.4.f_in, f32[2,16,32,128]{3,2,1,0:T(8,128)S(1)} %get-tuple-element.5.a_in), custom_call_target="tpu_custom_call" | custom-call | tf_op jit(solution)/shard_map/pallas_call | solution.py:1098

commit v4 on v3

--- a/solution.py
+++ b/solution.py
@@ -11,10 +11,11 @@
 SUB = 8
 RIM = 3
 LAG = 2
-LATE = 4
+LATE = 3
 HALVES = 2
 SLOW = 2.4
-DETOUR = ((0, 0), (0, 1), (1, 0), (1, 1))
+DETOUR = ((0, 0), (0, 1), (0, 2), (1, 0), (1, 1))
+SINGLE = ((0, 2),)
 HEAD, TAIL = 0, 1
 
 
@@ -716,8 +717,16 @@
     def far_send(a, lv, k, south):
         q = chunk_at(lv, k, south)
         if kind(a, lv, k) == "detour":
-            for h in range(HALVES):
-                out_copy(DETOUR.index((lv, k)), h, south).start()
+
+            def around():
+                for h in range(HALVES):
+                    out_copy(DETOUR.index((lv, k)), h, south).start()
+
+            if (lv, k) not in SINGLE:
+                around()
+            else:
+                pl.when(core == 1)(around)
+                pl.when(core == 0)(x_copy(a, q).start)
         elif kind(a, lv, k) == "direct":
             x_copy(a, q).start()
         else:
@@ -751,10 +760,17 @@
                 trim_take(a, lv, 0, south)
 
     def pass_on(south):
-        for i in range(len(DETOUR)):
-            for h in range(HALVES):
-                out_copy(i, h, south).wait_recv()
-                on_copy(i, h, south).start()
+        for i, spot in enumerate(DETOUR):
+
+            def hand():
+                for h in range(HALVES):
+                    out_copy(i, h, south).wait_recv()
+                    on_copy(i, h, south).start()
+
+            if spot in SINGLE:
+                pl.when(core == 1)(hand)
+            else:
+                hand()
 
     def send_level(a, lv):
         polar_half(lambda south: [far_send(a, lv, k, south) for k in range(per)])
@@ -802,6 +818,87 @@
         def _(r):
             for k, t in enumerate(zonal_taps(fractions[lv, first + r])):
                 taps[(lv * rows + r) * 6 + k] = t
+
+    def sweep(a, q, sink, sink_row, sign):
+        lv, r0 = chunks[q]
+        buf = gath[a][q]
+
+        @pl.loop(0, step)
+        def _(r):
+            buf[r, pl.ds(total_cells + cells, SUB), :] = buf[r, pl.ds(cells, SUB), :]
+            shift = shifts[lv, first + r0 + r]
+            if sign < 0:
+                start = lax.rem(2 * total_cells - shift - 3, total_cells)
+            else:
+                start = lax.rem(2 * total_cells + shift - 2, total_cells)
+            base = (lv * rows + r0 + r) * 6
+            w = [taps[base + k] for k in range(6)]
+            if sign > 0:
+                w = w[::-1]
+            for c in range(cells // SUB):
+                total = None
+                for k in range(6):
+                    term = w[k] * buf[r, pl.ds(start + c * SUB + k, SUB), :]
+                    total = term if total is None else total + term
+                sink[lv, sink_row + r0 + r, pl.ds(c * SUB, SUB), :] = total
+
+    def level_take(a, lv, k=0, south=True):
+        take(tr.at[lv], rc0.at[a, lv])
+
+    def finish(a, lv, k, south):
+        q = chunk_at(lv, k, south)
+        if kind(a, lv, k) == "trim":
+
+            @pl.when(core == a)
+            def _():
+                core_copy(a, q, 1).wait_recv()
+
+        else:
+            core_copy(a, q, 1).wait_recv()
+        if a == 0:
+            sweep(0, q, zb, RIM, -1)
+        else:
+            sweep(1, q, oa, 0, 1)
+
+    def polar_steps(a):
+        spots = [(lv, k) for lv in range(levels) for k in range(per)]
+        direct = [p for p in spots if kind(a, *p) != "detour"]
+        due = {p: i + SLOW for i, p in enumerate(direct)}
+        due.update({p: i for i, p in enumerate(DETOUR) if a == 1})
+        order = sorted(spots, key=lambda p: due[p])
+        steps = []
+        ready_levels = []
+        for i in range(nq + LAG):
+            if i < nq:
+                steps.append((relay, a) + order[i])
+            if i >= LAG:
+                lv, k = order[i - LAG]
+                if lv not in ready_levels:
+                    ready_levels.append(lv)
+                    steps.append((level_take, a, lv, k))
+                steps.append((finish, a, lv, k))
+        return steps
+
+    def polar_run(steps):
+        polar_half(lambda south: [step_[0](*step_[1:], south) for step_ in steps])
+
+    def middle_finish(a):
+        for lv in range(levels):
+            pack_take(a, lv)
+            level_take(a, lv)
+            for q in range(lv * per, (lv + 1) * per):
+                if a == 0:
+                    sweep(0, q, zb, RIM, -1)
+                else:
+                    sweep(1, q, oa, 0, 1)
+
+    take(tr, loc.at[levels + 1])
+
+    @pl.when(middle)
+    def _():
+        middle_finish(0)
+        for lv in range(levels):
+            lat_start(zb, 1, lv)
 
     for lv in range(levels):
         lat_wait(0, lv)
@@ -851,89 +948,13 @@
 
         send_level(1, lv)
 
-    def sweep(a, q, sink, sink_row, sign):
-        lv, r0 = chunks[q]
-        buf = gath[a][q]
-
-        @pl.loop(0, step)
-        def _(r):
-            buf[r, pl.ds(total_cells + cells, SUB), :] = buf[r, pl.ds(cells, SUB), :]
-            shift = shifts[lv, first + r0 + r]
-            if sign < 0:
-                start = lax.rem(2 * total_cells - shift - 3, total_cells)
-            else:
-                start = lax.rem(2 * total_cells + shift - 2, total_cells)
-            base = (lv * rows + r0 + r) * 6
-            w = [taps[base + k] for k in range(6)]
-            if sign > 0:
-                w = w[::-1]
-            for c in range(cells // SUB):
-                total = None
-                for k in range(6):
-                    term = w[k] * buf[r, pl.ds(start + c * SUB + k, SUB), :]
-                    total = term if total is None else total + term
-                sink[lv, sink_row + r0 + r, pl.ds(c * SUB, SUB), :] = total
-
-    def level_take(a, lv, k=0, south=True):
-        take(tr.at[lv], rc0.at[a, lv])
-
-    def finish(a, lv, k, south):
-        q = chunk_at(lv, k, south)
-        if kind(a, lv, k) == "trim":
-
-            @pl.when(core == a)
-            def _():
-                core_copy(a, q, 1).wait_recv()
-
-        else:
-            core_copy(a, q, 1).wait_recv()
-        if a == 0:
-            sweep(0, q, zb, RIM, -1)
-        else:
-            sweep(1, q, oa, 0, 1)
-
-    def polar_steps(a):
-        spots = [(lv, k) for lv in range(levels) for k in range(per)]
-        direct = [p for p in spots if kind(a, *p) != "detour"]
-        due = {p: i + SLOW for i, p in enumerate(direct)}
-        due.update({p: i for i, p in enumerate(DETOUR) if a == 1})
-        order = sorted(spots, key=lambda p: due[p])
-        steps = []
-        ready_levels = []
-        for i in range(nq + LAG):
-            if i < nq:
-                steps.append((relay, a) + order[i])
-            if i >= LAG:
-                lv, k = order[i - LAG]
-                if lv not in ready_levels:
-                    ready_levels.append(lv)
-                    steps.append((level_take, a, lv, k))
-                steps.append((finish, a, lv, k))
-        return steps
-
-    def polar_run(steps):
-        polar_half(lambda south: [step_[0](*step_[1:], south) for step_ in steps])
-
-    def middle_finish(a):
+
+    polar_run(polar_steps(0))
+
+    @pl.when(polar)
+    def _():
         for lv in range(levels):
-            pack_take(a, lv)
-            level_take(a, lv)
-            for q in range(lv * per, (lv + 1) * per):
-                if a == 0:
-                    sweep(0, q, zb, RIM, -1)
-                else:
-                    sweep(1, q, oa, 0, 1)
-
-    take(tr, loc.at[levels + 1])
-
-    polar_run(polar_steps(0))
-
-    @pl.when(middle)
-    def _():
-        middle_finish(0)
-
-    for lv in range(levels):
-        lat_start(zb, 1, lv)
+            lat_start(zb, 1, lv)
 
     @pl.when(middle)
     def _():
@@ -972,7 +993,12 @@
 
     polar_run(late[-LATE:])
 
-    take(lump(len(DETOUR)), sd.at[0])
+    for side in (HEAD, TAIL):
+
+        @pl.when(core == side)
+        def _():
+            take(lump(len(DETOUR) - (len(SINGLE) if side == 0 else 0)), sd.at[0])
+
     for k in range(2):
 
         @pl.when(lat > 0)
@@ -985,18 +1011,19 @@
 
     for a in range(2):
         take(tr, sc.at[a, 0])
-        straight = nq - levels - (len(DETOUR) if a == 1 else 0)
+        around = (len(DETOUR) - len(SINGLE), len(DETOUR)) if a == 1 else (0, 0)
+        straight = [nq - levels - m for m in around]
 
         @pl.when(jnp.logical_and(polar, core == a))
         def _():
-            take(lump(straight), sx.at[a])
+            take(lump(straight[a]), sx.at[a])
             take(lump(nq - levels), sc.at[a, 1])
             for w in range(2):
                 take(sendt.at[a, :, w, pl.ds(SUB, trims[a][1 + w][1])], st.at[w])
 
         @pl.when(jnp.logical_and(polar, core == 1 - a))
         def _():
-            take(lump(straight + levels), sx.at[a])
+            take(lump(straight[1 - a] + levels), sx.at[a])
             take(tr, sc.at[a, 1])
 
         for side in (HEAD, TAIL):

time: 23.6 us -> 23 us (0.975)
  Pallas kernels: 22.8 us -> 22.2 us
    pallas_call x1, Pallas kernels: 21.8 us -> 21.2 us  [local(): pl.pallas_call(functools.partial(body, dims), out_shape=(kept, kept), in_...]
where the time goes in v4:
time: 23 us; the launch traced here: 22.8 us
  Pallas kernels  22.2 us (97%)
  between operations  0.64 us (3%)
    pallas_call x1, Pallas kernels, local(): pl.pallas_call(functools.partial(body, dims), out_shape=(kept, kept), in_...  21.2 us
    pallas_call x1, Pallas kernels, local(): pl.pallas_call(store, out_shape=(final, final), in_specs=[vmem, vmem], ou...  0.99 us

profile of v4, /device:TPU:0, one launch (start us, length us, event | category | flops | bytes accessed | tf_op | source)
XLA Modules:
  0.0 22.8 jit_solution(10210874838692952112)
XLA Ops:
  0.6 21.2 %shard_map.68 = (f32[2,16,32,128]{3,2,1,0:T(8,128)S(1)}, f32[2,16,32,128]{3,2,1,0:T(8,128)S(1)}) custom-call(f32[2,16,32,128]{3,2,1,0:T(8,128)} %refs_0_.1, f32[2,16,32,128]{3,2,1,0:T(8,128)} %refs_1_.1, s32[2,64]{1,0:T(2,128)} %refs_2_.1, f32[2,64]{1,0:T(2,128)} %refs_3_.1, f32[2,32,64]{2,1,0:T(8,128)} %bitcast.1), custom_call_target="tpu_custom_call" | custom-call | tf_op jit(solution)/shard_map/pallas_call | solution.py:1114
  21.8 1.0 %shard_map.69 = (f32[2,16,32,128]{3,2,1,0:T(8,128)}, f32[2,16,32,128]{3,2,1,0:T(8,128)}) custom-call(f32[2,16,32,128]{3,2,1,0:T(8,128)S(1)} %get-tuple-element.4.f_in, f32[2,16,32,128]{3,2,1,0:T(8,128)S(1)} %get-tuple-element.5.a_in), custom_call_target="tpu_custom_call" | custom-call | tf_op jit(solution)/shard_map/pallas_call | solution.py:1125

commit v5 on v4

--- a/solution.py
+++ b/solution.py
@@ -432,7 +432,7 @@
     gath = (refs[7 : 7 + nq], refs[7 + nq : 7 + 2 * nq])
     zb, ab, vb, taps, shifts, fractions, mer, held = refs[7 + 2 * nq : 15 + 2 * nq]
     sendp, recvp, sendx, recvx, sendt, recvt = refs[15 + 2 * nq : 21 + 2 * nq]
-    loc, sx, sc, sd, st, sh, rf, rc0, rc1, rt, rh, ready = refs[21 + 2 * nq :]
+    loc, sx, sc, sd, st, sh, rf, rc0, rc1, rh, ready = refs[21 + 2 * nq :]
     total_cells = cells * n_lon
     total_rows = rows * n_lat
 
@@ -594,13 +594,14 @@
             lat=mate,
         )
 
-    def trim_copy(a, lv, w):
+    def trim_copy(a, lv, w, south):
+        q = chunk_at(lv, per - 1, south)
         long = trims[a][1 + w][1]
         return remote(
             sendt.at[a, lv, w, pl.ds(SUB, long)],
             recvt.at[a, lv, w, pl.ds(SUB, long)],
             st.at[w],
-            rt.at[a, lv],
+            rc1.at[a, q] if w else rf.at[a, q],
             lon=joint if w else beside,
         )
 
@@ -698,12 +699,12 @@
                 q, j = place_of(lv, rows - step + k, south)
                 for source, target in slots[k]:
                     sendt[a, lv, w, pl.ds(target, SUB), :] = gath[a][q][j, pl.ds(source, SUB), :]
-            trim_copy(a, lv, w).start()
+            trim_copy(a, lv, w, south).start()
 
     def trim_take(a, lv, w, south):
         near, *pair = trims[a]
         base = ring[1 - near] if w else 2 * cells
-        trim_copy(a, lv, w).wait_recv()
+        trim_copy(a, lv, w, south).wait_recv()
         for k in range(step):
             q, j = place_of(lv, rows - step + k, south)
             for source, target in pair[w][0][k]:
@@ -782,11 +783,12 @@
         for q in range(lv * per, (lv + 1) * per):
             core_copy(a, q, 0).start()
 
-    take(ad, loc.at[levels])
-    lat_start(ab, 0, 0)
     for lv in range(levels):
         take(tr.at[lv], loc.at[lv])
         send_level(0, lv)
+        if lv == 0:
+            take(ad, loc.at[levels])
+            lat_start(ab, 0, 0)
 
     @pl.when(lat == 0)
     def _():
@@ -1040,12 +1042,15 @@
 
 
 def store(f_in, a_in, f_out, a_out, sem):
-    one = pltpu.make_async_copy(f_in, f_out, sem.at[0])
-    two = pltpu.make_async_copy(a_in, a_out, sem.at[1])
-    one.start()
-    two.start()
-    one.wait()
-    two.wait()
+    part = max(1, f_in.shape[1] // 4)
+    pairs = ((f_in, f_out), (a_in, a_out))
+    for k, (source, target) in enumerate(pairs):
+        for lv in range(f_in.shape[0]):
+            for r0 in range(0, f_in.shape[1], part):
+                at = (lv, pl.ds(r0, part))
+                pltpu.make_async_copy(source.at[at], target.at[at], sem.at[k]).start()
+    for k, (source, target) in enumerate(pairs):
+        pltpu.make_async_copy(source, target, sem.at[k]).wait()
 
 
 def local(tracers, adjoint_in, shifts, fractions, meridional):
@@ -1094,7 +1099,6 @@
             dma((2, nq)),
             dma((2, levels)),
             dma((2, nq)),
-            dma((2, levels)),
             dma((2, levels)),
             pltpu.SemaphoreType.REGULAR,
         ]

time: 23 us -> 22.9 us (level)
  no operation moved by 1% of the time
where the time goes in v5:
time: 22.9 us; the launch traced here: 22.7 us
  Pallas kernels  22.1 us (97%)
  between operations  0.64 us (3%)
    pallas_call x1, Pallas kernels, local(): pl.pallas_call(functools.partial(body, dims), out_shape=(kept, kept), in_...  21.1 us
    pallas_call x1, Pallas kernels, local(): pl.pallas_call(store, out_shape=(final, final), in_specs=[vmem, vmem], ou...  0.97 us

profile of v5, /device:TPU:0, one launch (start us, length us, event | category | flops | bytes accessed | tf_op | source)
XLA Modules:
  0.0 22.7 jit_solution(14237817285663106341)
XLA Ops:
  0.6 21.1 %shard_map.68 = (f32[2,16,32,128]{3,2,1,0:T(8,128)S(1)}, f32[2,16,32,128]{3,2,1,0:T(8,128)S(1)}) custom-call(f32[2,16,32,128]{3,2,1,0:T(8,128)} %refs_0_.1, f32[2,16,32,128]{3,2,1,0:T(8,128)} %refs_1_.1, s32[2,64]{1,0:T(2,128)} %refs_2_.1, f32[2,64]{1,0:T(2,128)} %refs_3_.1, f32[2,32,64]{2,1,0:T(8,128)} %bitcast.1), custom_call_target="tpu_custom_call" | custom-call | tf_op jit(solution)/shard_map/pallas_call | solution.py:1118
  21.8 1.0 %shard_map.69 = (f32[2,16,32,128]{3,2,1,0:T(8,128)}, f32[2,16,32,128]{3,2,1,0:T(8,128)}) custom-call(f32[2,16,32,128]{3,2,1,0:T(8,128)S(1)} %get-tuple-element.4.f_in, f32[2,16,32,128]{3,2,1,0:T(8,128)S(1)} %get-tuple-element.5.a_in), custom_call_target="tpu_custom_call" | custom-call | tf_op jit(solution)/shard_map/pallas_call | solution.py:1129
